TPU v7x, 256 devices: a whole 4x4x8 slice. The times are simulated.
256 devices in a mesh: grp: 4 (over y), dev: 64 (over x, z, core).
Axes of the slice: x: 4, y: 4, z: 8, core: 2. Of those that a mesh axis runs over, the one named last changes fastest.
Arguments:
- pool_rows: bfloat16 [262144, 1024], P(('grp', 'dev')), may hold values from -6 to 6
- sample_index: int32 [262144], P(('grp', 'dev')), may hold values from 0 to 262143, as said below
- cluster_id: int32 [262144], P(('grp', 'dev')), may hold values from 0 to 511, as said below
- child_id: int32 [262144], P(('grp', 'dev')), may hold values from 0 to 7
- old_centroids: float32 [512, 8, 1024], P('dev'), may hold values from -6 to 6
Outputs:
- centroids: float32 [512, 8, 1024], P('dev')
- child_counts: int32 [512, 8], P('dev')
Inputs may be any that keep to these rules, and one draw needn't show every extreme that they name: Sample i takes a pool row of its own aligned block of 1024 rows: sample_index[i] // 1024 == i // 1024. `cluster_id`: in each aligned block of 1024 samples (the rows of one device) the 2 clusters o * 2 to o * 2 + 1 of any owner o are named at most 8 times together, and one cluster, the same in every block, is named exactly 8 times in every block.
All inputs are finite; a program needn't handle non-finite values.
Results may differ from a plain program's by a relative error of at most 0.0003.
Values may be sent and summed in bfloat16 or wider, within the bound.
A program may use at most 64 MiB of HBM per device.

v0:
```python
import math
import jax
import jax.numpy as jnp
from jax import lax
from jax.sharding import PartitionSpec as P


def side_by_side(arrays, axis, dim, along):
    widths = [math.prod(a.shape[along:]) for a in arrays]
    both = jnp.concatenate(
        [a.reshape(*a.shape[:along], w) for a, w in zip(arrays, widths)], axis=along
    )
    filled = lax.all_gather(both, axis, axis=dim, tiled=True)
    parts = jnp.split(filled, [sum(widths[:k]) for k in range(1, len(widths))], axis=along)
    return tuple(
        (b.reshape(*filled.shape[:along], *a.shape[along:]) for a, b in zip(arrays, parts))
    )


def segment_totals(rows, segment, segments):
    onehot = (jnp.arange(segments, dtype=jnp.int32)[:, None] == segment[None, :]).astype(
        jnp.bfloat16
    )
    sums = jnp.dot(onehot, rows, preferred_element_type=jnp.float32)
    counts = jnp.sum(onehot.astype(jnp.float32), axis=1)
    return (sums, counts)


def rank_within(keys_here):
    positions = jnp.arange(keys_here.shape[0], dtype=jnp.int32)
    matches = keys_here[:, None] == keys_here[None, :]
    earlier = positions[None, :] < positions[:, None]
    return jnp.sum(matches & earlier, axis=1)


def per_device(pool_rows, sample_index, cluster_id, child_id, old_centroids):
    rows_dev, row_width = pool_rows.shape
    block_clusters, kinds = (old_centroids.shape[0], old_centroids.shape[1])
    groups = lax.axis_size("grp")
    owners = lax.axis_size("dev")
    owned = block_clusters // groups
    clusters = block_clusters * owners
    most = 4 * rows_dev // clusters
    sample = pool_rows[sample_index % rows_dev]
    holder_table = cluster_id // owned
    slot_of = holder_table * most + rank_within(holder_table)
    total_slots = clusters // owned * most
    label_of = cluster_id % owned * kinds + child_id
    buffer = jnp.zeros((total_slots, row_width), jnp.bfloat16).at[slot_of].set(sample)
    labels = jnp.full((total_slots,), -1, jnp.int32).at[slot_of].set(label_of)
    shaped = buffer.reshape(owners, groups, most, row_width)
    shaped_labels = labels.reshape(owners, groups, most)
    arrived, arrived_labels = (
        lax.all_to_all(
            lax.all_to_all(shaped, "dev", split_axis=0, concat_axis=0, tiled=True),
            "grp",
            split_axis=1,
            concat_axis=1,
            tiled=True,
        ),
        lax.all_to_all(
            lax.all_to_all(shaped_labels, "dev", split_axis=0, concat_axis=0, tiled=True),
            "grp",
            split_axis=1,
            concat_axis=1,
            tiled=True,
        ),
    )
    sums, counts = segment_totals(
        arrived.reshape(-1, row_width), arrived_labels.reshape(-1), owned * kinds
    )
    group_index = lax.axis_index("grp")
    mine = lax.dynamic_slice_in_dim(old_centroids, group_index * owned, owned, 0)
    counts_owned = counts.reshape(owned, kinds)
    fresh = (sums.reshape(owned, kinds, row_width) + mine) / (counts_owned[:, :, None] + 1.0)
    centroids, new_counts = side_by_side((fresh, counts_owned), "grp", 0, 2)
    return (centroids, new_counts.astype(jnp.int32))


def solution(mesh):
    placed = (
        P(("grp", "dev"), None),
        P(("grp", "dev")),
        P(("grp", "dev")),
        P(("grp", "dev")),
        P("dev", None, None),
    )
    return jax.shard_map(
        per_device,
        mesh=mesh,
        in_specs=placed,
        out_specs=(P("dev", None, None), P("dev", None)),
        check_vma=False,
    )
```

profile of v0, /device:TPU:2, one launch (start us, length us, event | category | flops | bytes accessed | tf_op | source)
XLA Modules:
  0.0 222.8 jit_solution(11543515831146436987)
XLA Ops:
  0.6 0.8 add_select_fusion.2
  1.5 0.5 convert_reduce_fusion
  2.0 0.7 fusion.10
  2.8 4.3 %scatter_custom_fusion = s32[2048]{0:T(1024)S(1)} fusion(s32[1024]{0:T(1024)S(1)} %get-tuple-element.3, s32[1024]{0:T(1024)S(1)} %get-tuple-element.2, s32[]{:T(128)} %constant.47.clone.1), kind=kCustom, calls=%fused_computation.34 | custom fusion | bytes 8196 | tf_op jit(solution)/shard_map/scatter | solution.py:50
  7.1 0.8 reshape.46
  7.9 12.0 %all-to-all-start = ((s32[64,4,8]{2,1,0:T(4,128)}), s32[64,4,8]{2,1,0:T(4,128)S(1)}, u32[]{:S(2)}, u32[]{:S(2)}) async-start(s32[64,4,8]{2,1,0:T(4,128)} %reshape.46), calls=%async_computation | async-start | bytes 262144 | tf_op jit(solution)/shard_map/all_to_all | solution.py:62
  20.0 15.3 %scatter_custom_fusion.1 = bf16[2048,1024]{1,0:T(8,128)(2,1)} fusion(s32[1024]{0:T(1024)S(1)} %get-tuple-element.3, bf16[1024,1024]{1,0:T(8,128)(2,1)S(1)} %copy-done, s32[1024]{0:T(1024)S(1)} %get-tuple-element.4, bf16[]{:T(256)} %constant.52.clone.1), kind=kCustom, calls=%fused_computation.6 | custom fusion | bytes 4194306 | tf_op jit(solution)/shard_map/scatter | solution.py:49
  35.3 10.5 %all-to-all-start.2 = ((bf16[64,4,8,1024]{3,2,1,0:T(8,128)(2,1)}), bf16[64,4,8,1024]{3,2,1,0:T(8,128)(2,1)}, u32[]{:S(2)}, u32[]{:S(2)}) async-start(bf16[64,4,8,1024]{3,2,1,0:T(8,128)(2,1)} %bitcast.10), calls=%async_computation.2 | async-start | bytes 8388608 | tf_op jit(solution)/shard_map/all_to_all | solution.py:55
  45.9 0.7 reshape.85
  46.6 94.0 %all-to-all-done.2 = bf16[64,4,8,1024]{3,2,1,0:T(8,128)(2,1)} async-done(((bf16[64,4,8,1024]{3,2,1,0:T(8,128)(2,1)}), bf16[64,4,8,1024]{3,2,1,0:T(8,128)(2,1)}, u32[]{:S(2)}, u32[]{:S(2)}) %all-to-all-start.2) | async-done | bytes 4194336 | tf_op jit(solution)/shard_map/all_to_all | solution.py:55
  140.5 4.5 %all-to-all-start.1 = ((s32[4,1,512]{2,1,0:T(1,128)}), s32[4,1,512]{2,1,0:T(1,128)S(1)}, u32[]{:S(2)}, u32[]{:S(2)}) async-start(s32[4,1,512]{2,1,0:T(1,128)} %reshape.85), calls=%async_computation.1 | async-start | bytes 16384 | tf_op jit(solution)/shard_map/all_to_all | solution.py:61
  145.0 4.8 %copy.22 = bf16[64,4,8,1024]{3,2,0,1:T(8,128)(2,1)} copy(bf16[64,4,8,1024]{3,2,1,0:T(8,128)(2,1)} %all-to-all-done.2) | data formatting | bytes 8388608 | tf_op jit(solution)/shard_map/all_to_all | solution.py:55
  149.8 0.6 all-to-all-done.1
  150.3 4.9 %all-to-all-start.3 = ((bf16[64,4,8,1024]{3,2,0,1:T(8,128)(2,1)}), bf16[64,4,8,1024]{3,2,0,1:T(8,128)(2,1)}, u32[]{:S(2)}, u32[]{:S(2)}) async-start(bf16[64,4,8,1024]{3,2,0,1:T(8,128)(2,1)} %copy.22), calls=%async_computation.3 | async-start | bytes 8388608 | tf_op jit(solution)/shard_map/all_to_all | solution.py:54
  155.2 0.5 broadcast.69
  155.7 0.7 reduce
  156.6 0.2 eq.55
  156.7 0.1 convert_reduce_fusion.1
  157.1 47.7 %all-to-all-done.3 = bf16[64,4,8,1024]{3,2,0,1:T(8,128)(2,1)} async-done(((bf16[64,4,8,1024]{3,2,0,1:T(8,128)(2,1)}), bf16[64,4,8,1024]{3,2,0,1:T(8,128)(2,1)}, u32[]{:S(2)}, u32[]{:S(2)}) %all-to-all-start.3) | async-done | bytes 4194336 | tf_op jit(solution)/shard_map/all_to_all | solution.py:54
  204.7 2.6 %copy.23 = bf16[64,4,8,1024]{3,2,1,0:T(8,128)(2,1)S(1)} copy(bf16[64,4,8,1024]{3,2,0,1:T(8,128)(2,1)} %all-to-all-done.3) | data formatting | bytes 8388608 | tf_op jit(solution)/shard_map/all_to_all | solution.py:54
  207.4 1.5 fusion.4
  208.9 12.4 %all_gather.3 = f32[8,8,1025]{2,1,0:T(8,128)S(1)} all-gather(f32[2,8,1025]{2,1,0:T(8,128)S(1)} %pad_maximum_fusion), channel_id=1, replica_groups=mesh['grp'=4,'dev'=64] {'grp'}, dimensions={0}, use_global_device_ids=true | all-gather | bytes 328000 | tf_op jit(solution)/shard_map/all_gather | solution.py:13
  221.4 0.7 split.8
  222.2 0.6 convert_bitcast_fusion
  (13 shorter events, 0.6 us)
Async XLA Ops:
  0.6 19.3 %copy-start = (bf16[1024,1024]{1,0:T(8,128)(2,1)S(1)}, bf16[1024,1024]{1,0:T(8,128)(2,1)}, u32[]{:S(2)}) copy-start(bf16[1024,1024]{1,0:T(8,128)(2,1)} %param.5) | copy-start | bytes 6291460
  7.9 27.4 %all-to-all-start = ((s32[64,4,8]{2,1,0:T(4,128)}), s32[64,4,8]{2,1,0:T(4,128)S(1)}, u32[]{:S(2)}, u32[]{:S(2)}) async-start(s32[64,4,8]{2,1,0:T(4,128)} %reshape.46), calls=%async_computation | async-start | bytes 262144 | tf_op jit(solution)/shard_map/all_to_all | solution.py:62
  35.3 105.3 %all-to-all-start.2 = ((bf16[64,4,8,1024]{3,2,1,0:T(8,128)(2,1)}), bf16[64,4,8,1024]{3,2,1,0:T(8,128)(2,1)}, u32[]{:S(2)}, u32[]{:S(2)}) async-start(bf16[64,4,8,1024]{3,2,1,0:T(8,128)(2,1)} %bitcast.10), calls=%async_computation.2 | async-start | bytes 8388608 | tf_op jit(solution)/shard_map/all_to_all | solution.py:55
  140.5 9.8 %all-to-all-start.1 = ((s32[4,1,512]{2,1,0:T(1,128)}), s32[4,1,512]{2,1,0:T(1,128)S(1)}, u32[]{:S(2)}, u32[]{:S(2)}) async-start(s32[4,1,512]{2,1,0:T(1,128)} %reshape.85), calls=%async_computation.1 | async-start | bytes 16384 | tf_op jit(solution)/shard_map/all_to_all | solution.py:61
  150.3 54.4 %all-to-all-start.3 = ((bf16[64,4,8,1024]{3,2,0,1:T(8,128)(2,1)}), bf16[64,4,8,1024]{3,2,0,1:T(8,128)(2,1)}, u32[]{:S(2)}, u32[]{:S(2)}) async-start(bf16[64,4,8,1024]{3,2,0,1:T(8,128)(2,1)} %copy.22), calls=%async_computation.3 | async-start | bytes 8388608 | tf_op jit(solution)/shard_map/all_to_all | solution.py:54
where the time goes:
time: 223 us
  waiting for transfers between devices  142 us (64%)
  starting transfers between devices  31.9 us (14%)
  local copies, waits for them, and re-layouts  30.5 us (14%)
  blocking collectives  12.4 us (6%)
  other arithmetic  3.54 us (2%)
    all_to_all x1, waiting for transfers between devices, per_device(): lax.all_to_all(shaped, 'dev', split_axis=0, concat_axis=0, tiled=True)  94 us
    all_to_all x1, waiting for transfers between devices, per_device(): lax.all_to_all(lax.all_to_all(shaped, 'dev', split_axis=0, concat_axis=0,...  47.7 us
    scatter x1, local copies, waits for them, and re-layouts, per_device(): jnp.zeros((total_slots, row_width), jnp.bfloat16).at[slot_of].set(sample)  15.3 us
    all_gather x1, blocking collectives, side_by_side(): filled = lax.all_gather(both, axis, axis=dim, tiled=True)  12.4 us
    all_to_all x1, starting transfers between devices, per_device(): lax.all_to_all(shaped_labels, 'dev', split_axis=0, concat_axis=0, tiled=T...  12 us
    all_to_all x1, starting transfers between devices, per_device(): lax.all_to_all(shaped, 'dev', split_axis=0, concat_axis=0, tiled=True)  10.5 us
    all_to_all x1, starting transfers between devices, per_device(): lax.all_to_all(lax.all_to_all(shaped, 'dev', split_axis=0, concat_axis=0,...  4.86 us
    all_to_all x1, local copies, waits for them, and re-layouts, per_device(): lax.all_to_all(shaped, 'dev', split_axis=0, concat_axis=0, tiled=True)  4.75 us
  transfers between devices with their start and end apart: 4, of which 3 were waited for; matrix products, arithmetic and copies ran while one was open for 10% of the time, Pallas kernels for 0%

commit v1 on v0

--- a/solution.py
+++ b/solution.py
@@ -1,8 +1,36 @@
+import functools
 import math
 import jax
 import jax.numpy as jnp
 from jax import lax
 from jax.sharding import PartitionSpec as P
+
+
+def edge_push(v0, along_dim, panel):
+    extra, newest = (v0.shape[:along_dim], v0.shape[along_dim + 1 :])
+    return jnp.moveaxis(v0.reshape(*extra, panel, -1, *newest), along_dim, 0)
+
+
+def step_on_runs(row_data, d_out):
+    row_data = jnp.moveaxis(row_data, 0, d_out)
+    reply = row_data.shape
+    return row_data.reshape(*reply[:d_out], reply[d_out] * reply[d_out + 1], *reply[d_out + 2 :])
+
+
+def _touch_positions(array_in, shard_axis, obj, unit):
+    f_next, last = (jax.lax.axis_size(shard_axis), jax.lax.axis_index(shard_axis))
+    now = edge_push(array_in, obj, f_next)
+    by_place = [now[last]]
+    u = 1
+    while u < f_next:
+        out_arr = now[last ^ u]
+        by_place.append(jax.lax.ppermute(out_arr, shard_axis, [(i, i ^ u) for i in range(f_next)]))
+        u = u + 1
+    now = jnp.stack(by_place, axis=0)[last ^ jnp.arange(f_next)]
+    return step_on_runs(now, unit)
+
+
+produce_local_data = functools.partial(_touch_positions, shard_axis="grp", obj=1, unit=1)
 
 
 def side_by_side(arrays, axis, dim, along):
@@ -51,13 +79,7 @@
     shaped = buffer.reshape(owners, groups, most, row_width)
     shaped_labels = labels.reshape(owners, groups, most)
     arrived, arrived_labels = (
-        lax.all_to_all(
-            lax.all_to_all(shaped, "dev", split_axis=0, concat_axis=0, tiled=True),
-            "grp",
-            split_axis=1,
-            concat_axis=1,
-            tiled=True,
-        ),
+        produce_local_data(lax.all_to_all(shaped, "dev", split_axis=0, concat_axis=0, tiled=True)),
         lax.all_to_all(
             lax.all_to_all(shaped_labels, "dev", split_axis=0, concat_axis=0, tiled=True),
             "grp",

time: 223 us -> 212 us (0.951)
  waiting for transfers between devices: 142 us -> 127 us
  local copies, waits for them, and re-layouts: 30.5 us -> 34.6 us
  starting transfers between devices: 31.9 us -> 27.8 us
  other arithmetic: 3.54 us -> 7.14 us
    all_to_all x1 -> x0, waiting for transfers between devices: 47.7 us -> none  [per_device(): lax.all_to_all(lax.all_to_all(shaped, 'dev', split_axis=0, concat_axis=0,...]
    all_to_all x1, waiting for transfers between devices: 0.57 us -> 23.2 us  [per_device(): lax.all_to_all(lax.all_to_all(shaped_labels, 'dev', split_axis=0, concat_...]
    all_to_all x1, waiting for transfers between devices: 0.01 us -> 9.34 us  [per_device(): lax.all_to_all(shaped_labels, 'dev', split_axis=0, concat_axis=0, tiled=T...]
    all_to_all x2 -> x0, local copies, waits for them, and re-layouts: 7.38 us -> none  [the longest x1 4.75 us: per_device(): lax.all_to_all(shaped, 'dev', split_axis=0, concat_axis=0, tiled=True)]
    all_to_all x1, starting transfers between devices: 12 us -> 6.65 us  [per_device(): lax.all_to_all(shaped_labels, 'dev', split_axis=0, concat_axis=0, tiled=T...]
    gather x0 -> x1, local copies, waits for them, and re-layouts: none -> 4.97 us  [_touch_positions(): now = jnp.stack(by_place, axis=0)[last ^ jnp.arange(f_next)]]
    all_to_all x1 -> x0, starting transfers between devices: 4.86 us -> none  [per_device(): lax.all_to_all(lax.all_to_all(shaped, 'dev', split_axis=0, concat_axis=0,...]
    ppermute x0 -> x3, starting transfers between devices: none -> 4.7 us  [_touch_positions(): jax.lax.ppermute(out_arr, shard_axis, [(i, i ^ u) for i in range(f_next)])]
  transfers between devices with their start and end apart: 4 -> 6, of which waited for: 3 -> 3; matrix products, arithmetic and copies ran while one was open for 10% -> 4% of each run, Pallas kernels for 0% -> 0%
where the time goes in v1:
time: 212 us
  waiting for transfers between devices  127 us (60%)
  local copies, waits for them, and re-layouts  34.6 us (16%)
  starting transfers between devices  27.8 us (13%)
  blocking collectives  12.6 us (6%)
  other arithmetic  7.14 us (3%)
    all_to_all x1, waiting for transfers between devices, per_device(): lax.all_to_all(shaped, 'dev', split_axis=0, concat_axis=0, tiled=True)  94.7 us
    all_to_all x1, waiting for transfers between devices, per_device(): lax.all_to_all(lax.all_to_all(shaped_labels, 'dev', split_axis=0, concat_...  23.2 us
    scatter x1, local copies, waits for them, and re-layouts, per_device(): jnp.zeros((total_slots, row_width), jnp.bfloat16).at[slot_of].set(sample)  15.3 us
    all_gather x1, blocking collectives, side_by_side(): filled = lax.all_gather(both, axis, axis=dim, tiled=True)  12.6 us
    all_to_all x1, starting transfers between devices, per_device(): lax.all_to_all(shaped, 'dev', split_axis=0, concat_axis=0, tiled=True)  12.2 us
    all_to_all x1, waiting for transfers between devices, per_device(): lax.all_to_all(shaped_labels, 'dev', split_axis=0, concat_axis=0, tiled=T...  9.34 us
    all_to_all x1, starting transfers between devices, per_device(): lax.all_to_all(shaped_labels, 'dev', split_axis=0, concat_axis=0, tiled=T...  6.65 us
    gather x1, local copies, waits for them, and re-layouts, _touch_positions(): now = jnp.stack(by_place, axis=0)[last ^ jnp.arange(f_next)]  4.97 us
  transfers between devices with their start and end apart: 6, of which 3 were waited for; matrix products, arithmetic and copies ran while one was open for 4% of the time, Pallas kernels for 0%

profile of v1, /device:TPU:2, one launch (start us, length us, event | category | flops | bytes accessed | tf_op | source)
XLA Modules:
  0.0 211.7 jit_solution(5443434539753153519)
XLA Ops:
  0.6 0.8 add_select_fusion.2
  1.5 0.5 convert_reduce_fusion
  2.0 0.7 fusion.10
  2.8 15.3 %scatter_custom_fusion.1 = bf16[2048,1024]{1,0:T(8,128)(2,1)} fusion(s32[1024]{0:T(1024)S(1)} %get-tuple-element.7, bf16[1024,1024]{1,0:T(8,128)(2,1)S(1)} %copy-done, s32[1024]{0:T(1024)S(1)} %get-tuple-element.8, bf16[]{:T(256)} %constant.57.clone.1), kind=kCustom, calls=%fused_computation.8 | custom fusion | bytes 4194306 | tf_op jit(solution)/shard_map/scatter | solution.py:77
  18.1 12.2 %all-to-all-start.2 = ((bf16[64,4,8,1024]{3,2,1,0:T(8,128)(2,1)}), bf16[64,4,8,1024]{3,2,1,0:T(8,128)(2,1)}, u32[]{:S(2)}, u32[]{:S(2)}) async-start(bf16[64,4,8,1024]{3,2,1,0:T(8,128)(2,1)} %bitcast.28), calls=%async_computation.2 | async-start | bytes 8388608 | tf_op jit(solution)/shard_map/all_to_all | solution.py:82
  30.3 94.7 %all-to-all-done.2 = bf16[64,4,8,1024]{3,2,1,0:T(8,128)(2,1)} async-done(((bf16[64,4,8,1024]{3,2,1,0:T(8,128)(2,1)}), bf16[64,4,8,1024]{3,2,1,0:T(8,128)(2,1)}, u32[]{:S(2)}, u32[]{:S(2)}) %all-to-all-start.2) | async-done | bytes 4194336 | tf_op jit(solution)/shard_map/all_to_all | solution.py:82
  125.0 3.9 %dynamic-slice_bitcast_fusion.3 = (bf16[1,64,1,8,1024]{4,3,1,0,2:T(8,128)(2,1)S(1)}, bf16[64,1,8,1024]{3,2,0,1:T(8,128)(2,1)}, bf16[64,1,8,1024]{3,2,0,1:T(8,128)(2,1)}, bf16[64,1,8,1024]{3,2,0,1:T(8,128)(2,1)}) fusion(bf16[64,4,8,1024]{3,2,1,0:T(8,128)(2,1)} %all-to-all-done.2, s32[]{:T(128)S(6)} %select_n.53, s32[]{:T(128)S(6)} %select_n.55, ...), kind=kLoop, calls=%fused_computation.16 | loop fusion | bytes 8388624 | tf_op jit(solution)/shard_map/dynamic_slice | solution.py:23
  128.9 1.6 collective-permute-start
  130.5 2.9 %collective-permute-start.1 = (bf16[64,1,8,1024]{3,2,0,1:T(8,128)(2,1)}, bf16[64,1,8,1024]{3,2,0,1:T(8,128)(2,1)}, u32[]{:S(2)}, u32[]{:S(2)}) collective-permute-start(bf16[64,1,8,1024]{3,2,0,1:T(8,128)(2,1)} %get-tuple-element.3), channel_id=1, source_target_pairs={{0,128},{64,192},{128,0},{192,64},{1,129},{65,193},{129,1},{193,65... | collective-permute-start | bytes 3145736 | tf_op jit(solution)/shard_map/ppermute | solution.py:27
  133.6 4.3 %scatter_custom_fusion = s32[2048]{0:T(1024)S(1)} fusion(s32[1024]{0:T(1024)S(1)} %get-tuple-element.7, s32[1024]{0:T(1024)S(1)} %get-tuple-element.6, s32[]{:T(128)} %constant.52.clone.1), kind=kCustom, calls=%fused_computation.41 | custom fusion | bytes 8196 | tf_op jit(solution)/shard_map/scatter | solution.py:78
  138.0 0.8 reshape.75
  138.8 6.6 %all-to-all-start = ((s32[64,4,8]{2,1,0:T(4,128)}), s32[64,4,8]{2,1,0:T(4,128)S(1)}, u32[]{:S(2)}, u32[]{:S(2)}) async-start(s32[64,4,8]{2,1,0:T(4,128)} %reshape.75), calls=%async_computation | async-start | bytes 262144 | tf_op jit(solution)/shard_map/all_to_all | solution.py:84
  145.5 9.3 %all-to-all-done = s32[64,4,8]{2,1,0:T(4,128)S(1)} async-done(((s32[64,4,8]{2,1,0:T(4,128)}), s32[64,4,8]{2,1,0:T(4,128)S(1)}, u32[]{:S(2)}, u32[]{:S(2)}) %all-to-all-start) | async-done | bytes 8224 | tf_op jit(solution)/shard_map/all_to_all | solution.py:84
  154.9 0.7 reshape.123
  155.6 4.3 %all-to-all-start.1 = ((s32[4,1,512]{2,1,0:T(1,128)}), s32[4,1,512]{2,1,0:T(1,128)S(1)}, u32[]{:S(2)}, u32[]{:S(2)}) async-start(s32[4,1,512]{2,1,0:T(1,128)} %reshape.123), calls=%async_computation.1 | async-start | bytes 16384 | tf_op jit(solution)/shard_map/all_to_all | solution.py:83
  159.9 23.2 %all-to-all-done.1 = s32[4,1,512]{2,1,0:T(1,128)S(1)} async-done(((s32[4,1,512]{2,1,0:T(1,128)}), s32[4,1,512]{2,1,0:T(1,128)S(1)}, u32[]{:S(2)}, u32[]{:S(2)}) %all-to-all-start.1) | async-done | bytes 8224 | tf_op jit(solution)/shard_map/all_to_all | solution.py:83
  183.6 0.7 reduce
  185.0 3.6 %maximum_bitcast_fusion = bf16[4,64,8,1024]{3,2,1,0:T(8,128)(2,1)} fusion(bf16[1,64,1,8,1024]{4,3,1,0,2:T(8,128)(2,1)} %bitcast.4, bf16[1,64,1,8,1024]{4,3,1,0,2:T(8,128)(2,1)} %bitcast.3, bf16[1,64,1,8,1024]{4,3,1,0,2:T(8,128)(2,1)} %bitcast.2, bf16[1,64,1,8,1024]{4,3,1,0,2:T(8,128)(2,1)S(1)} %get-tuple-element.2), kind=kLoop, calls=%fused_computation.4 | loop fusion | flops 6291456 | bytes 8388608 | tf_op jit(solution)/shard_map/stack | solution.py:29
  188.5 5.0 %gather_fusion = bf16[4,64,8,1024]{3,2,1,0:T(8,128)(2,1)} fusion(bf16[4,64,8,1024]{3,2,1,0:T(8,128)(2,1)} %maximum_bitcast_fusion, s32[1024]{0:T(1024)S(1)} %pad_clamp_fusion), kind=kCustom, calls=%fused_computation.1 | custom fusion | bytes 8388624 | tf_op jit(solution)/shard_map/gather | solution.py:29
  193.5 2.6 %copy.31 = bf16[64,4,1,8,1024]{4,3,1,0,2:T(8,128)(2,1)S(1)} copy(bf16[64,4,1,8,1024]{4,3,0,1,2:T(8,128)(2,1)} %bitcast.29) | data formatting | bytes 8388608 | tf_op jit(solution)/shard_map/transpose | solution.py:15
  196.2 1.5 fusion.4
  197.7 12.6 %all_gather.3 = f32[8,8,1025]{2,1,0:T(8,128)S(1)} all-gather(f32[2,8,1025]{2,1,0:T(8,128)S(1)} %pad_maximum_fusion), channel_id=1, replica_groups=mesh['grp'=4,'dev'=64] {'grp'}, dimensions={0}, use_global_device_ids=true | all-gather | bytes 328000 | tf_op jit(solution)/shard_map/all_gather | solution.py:41
  210.3 0.7 split.8
  211.1 0.6 convert_bitcast_fusion
  (21 shorter events, 1.6 us)
Async XLA Ops:
  0.6 2.1 %copy-start = (bf16[1024,1024]{1,0:T(8,128)(2,1)S(1)}, bf16[1024,1024]{1,0:T(8,128)(2,1)}, u32[]{:S(2)}) copy-start(bf16[1024,1024]{1,0:T(8,128)(2,1)} %param.5) | copy-start | bytes 6291460
  18.1 107.0 %all-to-all-start.2 = ((bf16[64,4,8,1024]{3,2,1,0:T(8,128)(2,1)}), bf16[64,4,8,1024]{3,2,1,0:T(8,128)(2,1)}, u32[]{:S(2)}, u32[]{:S(2)}) async-start(bf16[64,4,8,1024]{3,2,1,0:T(8,128)(2,1)} %bitcast.28), calls=%async_computation.2 | async-start | bytes 8388608 | tf_op jit(solution)/shard_map/all_to_all | solution.py:82
  128.9 56.0 %collective-permute-start = (bf16[64,1,8,1024]{3,2,0,1:T(8,128)(2,1)}, bf16[64,1,8,1024]{3,2,0,1:T(8,128)(2,1)}, u32[]{:S(2)}, u32[]{:S(2)}) collective-permute-start(bf16[64,1,8,1024]{3,2,0,1:T(8,128)(2,1)} %get-tuple-element.4), channel_id=1, source_target_pairs={{0,64},{64,0},{128,192},{192,128},{1,65},{65,1},{129,193},{193,129... | collective-permute-start | bytes 3145736 | tf_op jit(solution)/shard_map/ppermute | solution.py:27
  130.5 54.4 %collective-permute-start.1 = (bf16[64,1,8,1024]{3,2,0,1:T(8,128)(2,1)}, bf16[64,1,8,1024]{3,2,0,1:T(8,128)(2,1)}, u32[]{:S(2)}, u32[]{:S(2)}) collective-permute-start(bf16[64,1,8,1024]{3,2,0,1:T(8,128)(2,1)} %get-tuple-element.3), channel_id=1, source_target_pairs={{0,128},{64,192},{128,0},{192,64},{1,129},{65,193},{129,1},{193,65... | collective-permute-start | bytes 3145736 | tf_op jit(solution)/shard_map/ppermute | solution.py:27
  133.4 51.5 %collective-permute-start.2 = (bf16[64,1,8,1024]{3,2,0,1:T(8,128)(2,1)}, bf16[64,1,8,1024]{3,2,0,1:T(8,128)(2,1)}, u32[]{:S(2)}, u32[]{:S(2)}) collective-permute-start(bf16[64,1,8,1024]{3,2,0,1:T(8,128)(2,1)} %get-tuple-element.5), channel_id=1, source_target_pairs={{0,192},{64,128},{128,64},{192,0},{1,193},{65,129},{129,65},{193,1... | collective-permute-start | bytes 3145736 | tf_op jit(solution)/shard_map/ppermute | solution.py:27
  138.8 16.0 %all-to-all-start = ((s32[64,4,8]{2,1,0:T(4,128)}), s32[64,4,8]{2,1,0:T(4,128)S(1)}, u32[]{:S(2)}, u32[]{:S(2)}) async-start(s32[64,4,8]{2,1,0:T(4,128)} %reshape.75), calls=%async_computation | async-start | bytes 262144 | tf_op jit(solution)/shard_map/all_to_all | solution.py:84
  155.6 27.5 %all-to-all-start.1 = ((s32[4,1,512]{2,1,0:T(1,128)}), s32[4,1,512]{2,1,0:T(1,128)S(1)}, u32[]{:S(2)}, u32[]{:S(2)}) async-start(s32[4,1,512]{2,1,0:T(1,128)} %reshape.123), calls=%async_computation.1 | async-start | bytes 16384 | tf_op jit(solution)/shard_map/all_to_all | solution.py:83
